TPU v7x, 256 devices: a whole 4x4x8 slice. The times are simulated.
256 devices in a mesh: seq: 64 (over y, x_lo, z), dp: 4 (over x_hi, core).
Axes of the slice: x: 4 (x_hi: 2, x_lo: 2; x = x_hi * 2 + x_lo), y: 4, z: 8, core: 2. Of those that a mesh axis runs over, the one named last changes fastest.
Arguments:
- queries: bfloat16 [4, 16384, 2048], P('dp', 'seq'), may hold values from -12 to 12
- keys: bfloat16 [4, 16384, 1024], P('dp', 'seq'), may hold values from -6 to 6
- values: bfloat16 [4, 16384, 1024], P('dp', 'seq'), may hold values from -6 to 6
- out_grad: bfloat16 [4, 16384, 1792], P('dp', 'seq'), may hold values from -6 to 6
- out_weight: bfloat16 [2048, 1792], P('seq'), may hold values from -0.125 to 0.125
- seq_len: int32 [4], P('dp'), may hold values from 4096 to 16384, as said below
Outputs:
- query_grad: bfloat16 [4, 16384, 2048], P('dp', 'seq')
- key_grad: bfloat16 [4, 16384, 1024], P('dp', 'seq')
- value_grad: bfloat16 [4, 16384, 1024], P('dp', 'seq')
- weight_grad: float32 [2048, 1792], P('seq')
- grad_rms: float32 [], replicated
Inputs may be any that keep to these rules, and one draw needn't show every extreme that they name: `seq_len`: at least one sequence has the full length 16384.
All inputs are finite; a program needn't handle non-finite values.
Results may differ from a plain program's by a relative error of at most 0.014.
Values may be sent and summed in bfloat16 or wider, within the bound.
No kernel may reach another device: no remote copies, remote signals or barrier semaphores. Data moves between devices by JAX's collectives and lax.ppermute only.
A program may use at most 128 MiB of HBM per device.

v0:
```python
import functools
import jax
import jax.numpy as jnp
from jax import lax
from jax.sharding import Mesh
from jax.sharding import PartitionSpec as P

HEADS = 8
KV_HEADS = 4
HEAD_DIM = 256
D_OUT = 1792
WINDOW = 512
TOK_DEV = 256
SEQ = ("seq_0", "seq_1", "seq_2")
DP = ("dp_0", "dp_1")
SEQ_DP = ("seq_0", "seq_1", "seq_2", "dp_0", "dp_1")
SCALE = 0.0625
CAP = 50.0


def shifted(value, axis, steps):
    count = lax.axis_size(axis)
    initial, last = (max(0, -steps), min(count, count - steps))
    return lax.ppermute(value, axis, [(source, source + steps) for source in range(initial, last)])


def copy_for_each(value, axis):
    size = lax.axis_size(axis)
    return lax.all_to_all(
        jnp.broadcast_to(value[None], (size, *value.shape)), axis, 0, 0, tiled=True
    )


def taken_together(value, axis):
    everything = copy_for_each(value, axis)
    return jnp.sum(everything.astype(jnp.float32), axis=0)


def over_axes(value, axes):
    return functools.reduce(lax.psum, axes, value)


def band_block(q_rows, k_rows, v_rows, g_rows, q_pos, k_pos):
    count = q_rows.shape[0]
    span = k_rows.shape[0]
    group = HEADS // KV_HEADS
    qh = q_rows.reshape(count, KV_HEADS, group, HEAD_DIM)
    kh = k_rows.reshape(span, KV_HEADS, HEAD_DIM)
    vh = v_rows.reshape(span, KV_HEADS, HEAD_DIM)
    gh = g_rows.reshape(count, KV_HEADS, group, HEAD_DIM)
    raw = jnp.einsum("tkgd,jkd->kgtj", qh, kh, preferred_element_type=jnp.float32) * SCALE
    capped = CAP * jnp.tanh(raw / CAP)
    allowed = (
        (k_pos[None, :] >= 0)
        & (k_pos[None, :] <= q_pos[:, None])
        & (k_pos[None, :] > q_pos[:, None] - WINDOW)
    )
    expo = jnp.where(allowed, jnp.exp(capped), jnp.zeros((), jnp.float32))
    probs = expo / jnp.sum(expo, axis=-1, keepdims=True)
    probs_b = probs.astype(jnp.bfloat16)
    attn = jnp.einsum("kgtj,jkd->tkgd", probs_b, vh, preferred_element_type=jnp.float32).astype(
        jnp.bfloat16
    )
    delta = jnp.einsum("tkgd,tkgd->kgt", gh, attn, preferred_element_type=jnp.float32)[..., None]
    dprob = jnp.einsum("tkgd,jkd->kgtj", gh, vh, preferred_element_type=jnp.float32)
    dscore = (probs * (dprob - delta) * (1.0 - (capped / CAP) ** 2) * SCALE).astype(jnp.bfloat16)
    dq = jnp.einsum("kgtj,jkd->tkgd", dscore, kh, preferred_element_type=jnp.float32).reshape(
        count, -1
    )
    dk = jnp.einsum("kgtj,tkgd->jkd", dscore, qh, preferred_element_type=jnp.float32).reshape(
        span, -1
    )
    dv = jnp.einsum("kgtj,tkgd->jkd", probs_b, gh, preferred_element_type=jnp.float32).reshape(
        span, -1
    )
    return (dq, dk, dv, attn.reshape(count, -1))


def shards(queries, keys, values, out_grad, out_weight, seq_len):
    q_rows = queries[0]
    k_rows = keys[0]
    v_rows = values[0]
    length = seq_len[0]
    seq_devices = lax.axis_size(SEQ)
    rep_devices = lax.axis_size(DP)
    start = lax.axis_index(SEQ) * TOK_DEV
    positions = start + jnp.arange(TOK_DEV, dtype=jnp.int32)
    valid = positions < length
    masked = jnp.where(valid[:, None], out_grad[0], jnp.zeros((), jnp.bfloat16))
    grad_attn = lax.dot_general(
        masked,
        lax.all_gather(out_weight, SEQ, axis=0, tiled=True),
        (((1,), (1,)), ((), ())),
        preferred_element_type=jnp.float32,
    ).astype(jnp.bfloat16)
    reach = (WINDOW + TOK_DEV - 2) // TOK_DEV
    lead = reach * TOK_DEV
    key_parts = []
    val_parts = []
    for back in range(reach, 0, -1):
        earlier_k, earlier_v = shifted((k_rows, v_rows), SEQ, back)
        key_parts.append(earlier_k)
        val_parts.append(earlier_v)
    key_block = jnp.concatenate(key_parts + [k_rows], 0)
    val_block = jnp.concatenate(val_parts + [v_rows], 0)
    k_pos = start - lead + jnp.arange(lead + TOK_DEV, dtype=jnp.int32)
    dq_raw, dk_all, dv_all, attn = band_block(
        q_rows, key_block, val_block, grad_attn, positions, k_pos
    )
    dk_raw = dk_all[lead:]
    dv_raw = dv_all[lead:]
    for back in range(1, reach + 1):
        first = (reach - back) * TOK_DEV
        later_k, later_v = (
            shifted(dk_all[first : first + TOK_DEV].astype(jnp.bfloat16), SEQ, -back).astype(
                jnp.float32
            ),
            shifted(dv_all[first : first + TOK_DEV].astype(jnp.bfloat16), SEQ, -back).astype(
                jnp.float32
            ),
        )
        dk_raw = dk_raw + later_k
        dv_raw = dv_raw + later_v
    width = HEADS * HEAD_DIM
    part = lax.psum_scatter(
        lax.dot_general(attn, masked, (((0,), (0,)), ((), ())), preferred_element_type=jnp.float32),
        SEQ,
        scatter_dimension=0,
        tiled=True,
    )
    weight_raw = taken_together(part.astype(jnp.bfloat16), DP).astype(jnp.float32)
    weight_sq = jnp.sum(weight_raw * weight_raw) / rep_devices
    own_count = jnp.clip(length - start, 0, TOK_DEV)
    slots = TOK_DEV * seq_devices * rep_devices
    entries = slots * (HEADS + 2 * KV_HEADS) * HEAD_DIM + width * D_OUT
    act_sq = jnp.sum(dq_raw * dq_raw) + jnp.sum(dk_raw * dk_raw) + jnp.sum(dv_raw * dv_raw)
    total, act_total, weight_total = (
        over_axes(own_count.astype(jnp.float32), SEQ_DP),
        over_axes(act_sq, SEQ_DP),
        over_axes(weight_sq, SEQ_DP),
    )
    act_scale = slots / total
    weight_scale = lax.rsqrt(total)
    dq_s = dq_raw * act_scale
    dk_s = dk_raw * act_scale
    dv_s = dv_raw * act_scale
    squares = act_total * (act_scale * act_scale) + weight_total * (weight_scale * weight_scale)
    grad_rms = jnp.sqrt(squares / entries)
    weight_grad = weight_raw * weight_scale
    return (
        dq_s.astype(jnp.bfloat16)[None],
        dk_s.astype(jnp.bfloat16)[None],
        dv_s.astype(jnp.bfloat16)[None],
        weight_grad,
        grad_rms,
    )


def solution(mesh):
    split = Mesh(mesh.devices.reshape(4, 2, 8, 2, 2), ("seq_0", "seq_1", "seq_2", "dp_0", "dp_1"))
    placed = (
        P(DP, SEQ, None),
        P(DP, SEQ, None),
        P(DP, SEQ, None),
        P(DP, SEQ, None),
        P(SEQ, None),
        P(DP),
    )
    return jax.shard_map(
        shards,
        mesh=split,
        in_specs=placed,
        out_specs=(P(DP, SEQ, None), P(DP, SEQ, None), P(DP, SEQ, None), P(SEQ, None), P()),
        check_vma=False,
    )
```

profile of v0, /device:TPU:1, one launch (start us, length us, event | category | flops | bytes accessed | tf_op | source)
XLA Modules:
  0.0 783.0 jit_solution(6166765927309741051)
XLA Ops:
  9.2 5.2 collective-permute-start.3
  14.4 4.9 collective-permute-start.2
  20.5 5.6 collective-permute-start.1
  26.1 2.3 collective-permute-start
  32.0 2.2 copy.64
  34.2 8.4 %collective-permute-done.2 = bf16[256,1024]{0,1:T(8,128)(2,1)} collective-permute-done((bf16[256,1024]{0,1:T(8,128)(2,1)S(1)}, bf16[256,1024]{0,1:T(8,128)(2,1)}, u32[]{:S(2)}, u32[]{:S(2)}) %collective-permute-start.2) | collective-permute-done | bytes 524320 | tf_op jit(solution)/shard_map/ppermute | solution.py:24
  44.6 22.7 %collective-permute-done.1 = bf16[256,1024]{0,1:T(8,128)(2,1)} collective-permute-done((bf16[256,1024]{0,1:T(8,128)(2,1)S(1)}, bf16[256,1024]{0,1:T(8,128)(2,1)}, u32[]{:S(2)}, u32[]{:S(2)}) %collective-permute-start.1) | collective-permute-done | bytes 524320 | tf_op jit(solution)/shard_map/ppermute | solution.py:24
  68.6 17.5 %collective-permute-done = bf16[256,1024]{0,1:T(8,128)(2,1)} collective-permute-done((bf16[256,1024]{0,1:T(8,128)(2,1)S(1)}, bf16[256,1024]{0,1:T(8,128)(2,1)}, u32[]{:S(2)}, u32[]{:S(2)}) %collective-permute-start) | collective-permute-done | bytes 524320 | tf_op jit(solution)/shard_map/ppermute | solution.py:24
  89.4 2.6 copy-done
  93.8 195.2 %all-gather.2.cloned.1.call-done = bf16[2048,1792]{1,0:T(8,128)(2,1)} async-done(((bf16[32,1792]{1,0:T(8,128)(2,1)}), bf16[2048,1792]{1,0:T(8,128)(2,1)}) %all-gather.2.cloned.1.call-update) | async-done | bytes 7340048 | tf_op jit(solution)/shard_map/all_gather | solution.py:92
  289.0 6.5 convolution_convert_fusion
  295.5 2.6 reshape.85
  298.1 3.3 bitcast_convert_fusion
  301.4 4.1 copy.91
  305.6 3.2 multiply_reduce_fusion
  308.8 7.4 fusion.6
  316.2 3.6 copy.76
  319.8 6.8 fusion.1
  326.7 2.6 fusion.27
  337.1 3.9 fusion.28
  349.0 5.4 multiply_reduce_fusion.1
  354.3 302.3 %reduce-scatter.2.cloned.1.call-done = f32[32,1792]{1,0:T(8,128)} async-done(((f32[2048,1792]{1,0:T(8,128)}), f32[32,1792]{1,0:T(8,128)}) %reduce-scatter.2.cloned.1.call-update) | async-done | bytes 229392 | tf_op jit(solution)/shard_map/reduce_scatter | solution.py:125
  658.4 55.7 %all-to-all-start = ((bf16[4,32,1792]{2,1,0:T(8,128)(2,1)}), bf16[4,32,1792]{2,1,0:T(8,128)(2,1)S(1)}, u32[]{:S(2)}, u32[]{:S(2)}) async-start(bf16[4,32,1792]{2,1,0:T(8,128)(2,1)} %broadcast_in_dim.53), calls=%async_computation.1 | async-start | bytes 917504 | tf_op jit(solution)/shard_map/all_to_all | solution.py:29
  714.2 2.1 multiply_reduce_fusion.3
  720.3 2.5 all-to-all-done
  724.2 6.5 all-reduce.1
  730.7 4.4 all-reduce.4
  735.1 11.4 %all-reduce = (f32[]{:T(128)}, f32[]{:T(128)}, f32[]{:T(128)}) all-reduce(f32[]{:T(128)} %get-tuple-element.32, f32[]{:T(128)} %get-tuple-element.33, f32[]{:T(128)} %get-tuple-element.34), channel_id=1, replica_groups=mesh['seq_0'=4,'seq_1'=2,'seq_2'=8,'dp_0'=2,'dp_1'=2] {'seq_2'}, use_global_device_ids=true, to_apply=%region_3.4 | all-reduce | flops 3 | bytes 24 | tf_op jit(solution)/shard_map/psum | solution.py:40
  746.5 5.9 all-reduce.3
  752.4 11.5 %all-reduce.2 = (f32[]{:T(128)}, f32[]{:T(128)}, f32[]{:T(128)}) all-reduce(f32[]{:T(128)} %get-tuple-element.29, f32[]{:T(128)} %get-tuple-element.30, f32[]{:T(128)} %get-tuple-element.31), channel_id=1, replica_groups=mesh['seq_0'=4,'seq_1'=2,'seq_2'=8,'dp_0'=2,'dp_1'=2] {'dp_1'}, use_global_device_ids=true, to_apply=%region_5.6 | all-reduce | flops 3 | bytes 24 | tf_op jit(solution)/shard_map/psum | solution.py:40
  770.6 2.2 fusion.14
  772.8 2.2 fusion.13
  (63 shorter events, 38.6 us)
Async XLA Ops:
  7.2 23.9 %copy-start.4 = (bf16[1,256,2048]{2,1,0:T(8,128)(2,1)S(1)}, bf16[1,256,2048]{2,1,0:T(8,128)(2,1)}, u32[]{:S(2)}) copy-start(bf16[1,256,2048]{2,1,0:T(8,128)(2,1)} %param.6) | copy-start | bytes 3145732
  7.2 281.8 %all-gather.2.cloned.1.call-start = ((), (), s32[]{:S(2)}) async-start(), calls=%async_computation.2 | async-start | bytes 7454720 | tf_op jit(solution)/shard_map/all_gather | solution.py:92
  7.9 648.8 %reduce-scatter.2.cloned.1.call-start = ((), (), s32[]{:S(2)}) async-start(), calls=%async_computation.3 | async-start | bytes 14909440 | tf_op jit(solution)/shard_map/reduce_scatter | solution.py:125
  9.2 22.8 %collective-permute-start.3 = (bf16[256,1024]{0,1:T(8,128)(2,1)S(1)}, bf16[256,1024]{0,1:T(8,128)(2,1)}, u32[]{:S(2)}, u32[]{:S(2)}) collective-permute-start(bf16[256,1024]{0,1:T(8,128)(2,1)S(1)} %bitcast.113), channel_id=1, source_target_pairs={{0,4},{4,8},{8,12},{12,16},{16,20},{20,24},{24,28},{28,32},{32,36}... | collective-permute-start | bytes 1572872 | tf_op jit(solution)/shard_map/ppermute | solution.py:24
  14.4 28.2 %collective-permute-start.2 = (bf16[256,1024]{0,1:T(8,128)(2,1)S(1)}, bf16[256,1024]{0,1:T(8,128)(2,1)}, u32[]{:S(2)}, u32[]{:S(2)}) collective-permute-start(bf16[256,1024]{0,1:T(8,128)(2,1)S(1)} %bitcast.114), channel_id=1, source_target_pairs={{0,8},{4,12},{8,16},{12,20},{16,24},{20,28},{24,32},{28,36},{32,40... | collective-permute-start | bytes 1572872 | tf_op jit(solution)/shard_map/ppermute | solution.py:24
  20.5 46.9 %collective-permute-start.1 = (bf16[256,1024]{0,1:T(8,128)(2,1)S(1)}, bf16[256,1024]{0,1:T(8,128)(2,1)}, u32[]{:S(2)}, u32[]{:S(2)}) collective-permute-start(bf16[256,1024]{0,1:T(8,128)(2,1)S(1)} %bitcast.110), channel_id=1, source_target_pairs={{0,4},{4,8},{8,12},{12,16},{16,20},{20,24},{24,28},{28,32},{32,36}... | collective-permute-start | bytes 1572872 | tf_op jit(solution)/shard_map/ppermute | solution.py:24
  26.1 60.1 %collective-permute-start = (bf16[256,1024]{0,1:T(8,128)(2,1)S(1)}, bf16[256,1024]{0,1:T(8,128)(2,1)}, u32[]{:S(2)}, u32[]{:S(2)}) collective-permute-start(bf16[256,1024]{0,1:T(8,128)(2,1)S(1)} %bitcast.111), channel_id=1, source_target_pairs={{0,8},{4,12},{8,16},{12,20},{16,24},{20,28},{24,32},{28,36},{32,40... | collective-permute-start | bytes 1572872 | tf_op jit(solution)/shard_map/ppermute | solution.py:24
  31.6 57.8 %copy-start.1 = (bf16[1,256,2048]{1,2,0:T(8,128)(2,1)}, bf16[1,256,2048]{1,2,0:T(8,128)(2,1)S(1)}, u32[]{:S(2)}) copy-start(bf16[1,256,2048]{1,2,0:T(8,128)(2,1)S(1)} %copy.102) | copy-start | bytes 3145732
  31.6 55.8 %copy-start.6 = (bf16[256,4,256]{2,0,1:T(8,128)(2,1)S(1)}, bf16[256,4,256]{2,0,1:T(8,128)(2,1)}, u32[]{:S(2)}) copy-start(bf16[256,4,256]{2,0,1:T(8,128)(2,1)} %copy.59) | copy-start | bytes 1572868
  68.6 20.8 %copy-start.7 = (bf16[256,4,256]{2,0,1:T(8,128)(2,1)}, bf16[256,4,256]{2,0,1:T(8,128)(2,1)S(1)}, u32[]{:S(2)}) copy-start(bf16[256,4,256]{2,0,1:T(8,128)(2,1)S(1)} %copy.58) | copy-start | bytes 1572868
  87.4 2.0 copy-start.8
  89.4 2.6 copy-start
  305.6 3.2 copy-start.5
  319.8 6.9 copy-start.2
  326.7 2.6 copy-start.3
  334.5 379.7 %collective-permute-start.5 = (bf16[256,1024]{1,0:T(8,128)(2,1)}, bf16[256,1024]{1,0:T(8,128)(2,1)}, u32[]{:S(2)}, u32[]{:S(2)}) collective-permute-start(bf16[256,1024]{1,0:T(8,128)(2,1)} %copy.75), channel_id=1, source_target_pairs={{8,0},{12,4},{16,8},{20,12},{24,16},{28,20},{32,24},{36,28},{40,32... | collective-permute-start | bytes 1572872 | tf_op jit(solution)/shard_map/ppermute | solution.py:24
  335.8 378.4 %collective-permute-start.4 = (bf16[256,1024]{1,0:T(8,128)(2,1)}, bf16[256,1024]{1,0:T(8,128)(2,1)}, u32[]{:S(2)}, u32[]{:S(2)}) collective-permute-start(bf16[256,1024]{1,0:T(8,128)(2,1)} %copy.73), channel_id=1, source_target_pairs={{4,0},{8,4},{12,8},{16,12},{20,16},{24,20},{28,24},{32,28},{36,32}... | collective-permute-start | bytes 1572872 | tf_op jit(solution)/shard_map/ppermute | solution.py:24
  343.1 374.5 %collective-permute-start.7 = (bf16[256,1024]{1,0:T(8,128)(2,1)}, bf16[256,1024]{1,0:T(8,128)(2,1)}, u32[]{:S(2)}, u32[]{:S(2)}) collective-permute-start(bf16[256,1024]{1,0:T(8,128)(2,1)} %copy.80), channel_id=1, source_target_pairs={{8,0},{12,4},{16,8},{20,12},{24,16},{28,20},{32,24},{36,28},{40,32... | collective-permute-start | bytes 1572872 | tf_op jit(solution)/shard_map/ppermute | solution.py:24
  344.4 373.2 %collective-permute-start.6 = (bf16[256,1024]{1,0:T(8,128)(2,1)}, bf16[256,1024]{1,0:T(8,128)(2,1)}, u32[]{:S(2)}, u32[]{:S(2)}) collective-permute-start(bf16[256,1024]{1,0:T(8,128)(2,1)} %copy.78), channel_id=1, source_target_pairs={{4,0},{8,4},{12,8},{16,12},{20,16},{24,20},{28,24},{32,28},{36,32}... | collective-permute-start | bytes 1572872 | tf_op jit(solution)/shard_map/ppermute | solution.py:24
  658.4 64.4 %all-to-all-start = ((bf16[4,32,1792]{2,1,0:T(8,128)(2,1)}), bf16[4,32,1792]{2,1,0:T(8,128)(2,1)S(1)}, u32[]{:S(2)}, u32[]{:S(2)}) async-start(bf16[4,32,1792]{2,1,0:T(8,128)(2,1)} %broadcast_in_dim.53), calls=%async_computation.1 | async-start | bytes 917504 | tf_op jit(solution)/shard_map/all_to_all | solution.py:29
Sparse Core Ops, SparseCore 0:
  9.8 279.1 all-gather.1
  316.3 340.3 reduce-scatter.1
where the time goes:
time: 784 us; the launch traced here: 783 us
  waiting for transfers between devices  549 us (70%)
  starting transfers between devices  78.9 us (10%)
  blocking collectives  39.8 us (5%)
  matrix products  37.8 us (5%)
  local copies, waits for them, and re-layouts  37.5 us (5%)
  between operations  21.5 us (3%)
  other arithmetic  18.2 us (2%)
    reduce_scatter x1, waiting for transfers between devices, shards(): lax.psum_scatter(lax.dot_general(attn, masked, (((0,), (0,)), ((), ())),...  302 us
    all_gather x1, waiting for transfers between devices, shards(): lax.all_gather(out_weight, SEQ, axis=0, tiled=True)  195 us
    all_to_all x1, starting transfers between devices, copy_for_each(): lax.all_to_all(jnp.broadcast_to(value[None], (size, *value.shape)), axis,...  55.7 us
    ppermute x8, waiting for transfers between devices, shifted(): lax.ppermute(value, axis, [(source, source + steps) for source in range(i...  48.6 us
    psum x5, blocking collectives, over_axes(): return functools.reduce(lax.psum, axes, value)  39.8 us
    ppermute x8, starting transfers between devices, shifted(): lax.ppermute(value, axis, [(source, source + steps) for source in range(i...  23.1 us
  transfers between devices with their start and end apart: 11, of which 6 were waited for; matrix products, arithmetic and copies ran while one was open for 7% of the time, Pallas kernels for 0%

commit v1 on v0

--- a/solution.py
+++ b/solution.py
@@ -89,7 +89,9 @@
     masked = jnp.where(valid[:, None], out_grad[0], jnp.zeros((), jnp.bfloat16))
     grad_attn = lax.dot_general(
         masked,
-        lax.all_gather(out_weight, SEQ, axis=0, tiled=True),
+        jnp.concatenate(
+            lax.all_to_all(jnp.stack([out_weight] * lax.axis_size(SEQ)), SEQ, 0, 0), axis=0
+        ),
         (((1,), (1,)), ((), ())),
         preferred_element_type=jnp.float32,
     ).astype(jnp.bfloat16)

time: 784 us -> 738 us (0.941)
  waiting for transfers between devices: 549 us -> 500 us
    all_gather x1 -> x0, waiting for transfers between devices: 195 us -> none  [shards(): lax.all_gather(out_weight, SEQ, axis=0, tiled=True)]
    ppermute x8, waiting for transfers between devices: 48.6 us -> 195 us  [shifted(): lax.ppermute(value, axis, [(source, source + steps) for source in range(i...]
    all_to_all x1, starting transfers between devices: 55.7 us -> 41.1 us  [copy_for_each(): lax.all_to_all(jnp.broadcast_to(value[None], (size, *value.shape)), axis,...]
    all_to_all x0 -> x1, starting transfers between devices: none -> 13.9 us  [shards(): lax.all_to_all(jnp.stack([out_weight] * lax.axis_size(SEQ)), SEQ, 0, 0)]
where the time goes in v1:
time: 738 us; the launch traced here: 736 us
  waiting for transfers between devices  500 us (68%)
  starting transfers between devices  75.1 us (10%)
  blocking collectives  42.2 us (6%)
  local copies, waits for them, and re-layouts  41 us (6%)
  matrix products  37.7 us (5%)
  between operations  21.5 us (3%)
  other arithmetic  18.2 us (2%)
    reduce_scatter x1, waiting for transfers between devices, shards(): lax.psum_scatter(lax.dot_general(attn, masked, (((0,), (0,)), ((), ())),...  303 us
    ppermute x8, waiting for transfers between devices, shifted(): lax.ppermute(value, axis, [(source, source + steps) for source in range(i...  195 us
    psum x5, blocking collectives, over_axes(): return functools.reduce(lax.psum, axes, value)  42.2 us
    all_to_all x1, starting transfers between devices, copy_for_each(): lax.all_to_all(jnp.broadcast_to(value[None], (size, *value.shape)), axis,...  41.1 us
    ppermute x8, starting transfers between devices, shifted(): lax.ppermute(value, axis, [(source, source + steps) for source in range(i...  20 us
  transfers between devices with their start and end apart: 11, of which 6 were waited for; matrix products, arithmetic and copies ran while one was open for 7% of the time, Pallas kernels for 0%

profile of v1, /device:TPU:1, one launch (start us, length us, event | category | flops | bytes accessed | tf_op | source)
XLA Modules:
  0.0 736.2 jit_solution(4632654878203520014)
XLA Ops:
  7.2 4.8 stack.2
  12.0 13.9 %all-to-all-start = ((bf16[64,32,1792]{2,1,0:T(8,128)(2,1)}), bf16[64,32,1792]{2,1,0:T(8,128)(2,1)}, u32[]{:S(2)}, u32[]{:S(2)}) async-start(bf16[64,32,1792]{2,1,0:T(8,128)(2,1)} %stack.2), calls=%async_computation | async-start | bytes 14680064 | tf_op jit(solution)/shard_map/all_to_all | solution.py:93
  26.2 3.7 collective-permute-start.1
  29.9 4.0 collective-permute-start
  34.1 5.1 collective-permute-start.3
  44.0 149.4 %collective-permute-done.1 = bf16[256,1024]{0,1:T(8,128)(2,1)} collective-permute-done((bf16[256,1024]{0,1:T(8,128)(2,1)S(1)}, bf16[256,1024]{0,1:T(8,128)(2,1)}, u32[]{:S(2)}, u32[]{:S(2)}) %collective-permute-start.1) | collective-permute-done | bytes 524320 | tf_op jit(solution)/shard_map/ppermute | solution.py:24
  194.7 15.3 %collective-permute-done = bf16[256,1024]{0,1:T(8,128)(2,1)} collective-permute-done((bf16[256,1024]{0,1:T(8,128)(2,1)S(1)}, bf16[256,1024]{0,1:T(8,128)(2,1)}, u32[]{:S(2)}, u32[]{:S(2)}) %collective-permute-start) | collective-permute-done | bytes 524320 | tf_op jit(solution)/shard_map/ppermute | solution.py:24
  211.2 15.9 %collective-permute-done.3 = bf16[256,1024]{0,1:T(8,128)(2,1)} collective-permute-done((bf16[256,1024]{0,1:T(8,128)(2,1)S(1)}, bf16[256,1024]{0,1:T(8,128)(2,1)}, u32[]{:S(2)}, u32[]{:S(2)}) %collective-permute-start.3) | collective-permute-done | bytes 524320 | tf_op jit(solution)/shard_map/ppermute | solution.py:24
  229.2 14.6 %collective-permute-done.2 = bf16[256,1024]{0,1:T(8,128)(2,1)} collective-permute-done((bf16[256,1024]{0,1:T(8,128)(2,1)S(1)}, bf16[256,1024]{0,1:T(8,128)(2,1)}, u32[]{:S(2)}, u32[]{:S(2)}) %collective-permute-start.2) | collective-permute-done | bytes 524320 | tf_op jit(solution)/shard_map/ppermute | solution.py:24
  247.8 2.6 copy-done
  252.2 6.5 convolution_convert_fusion
  258.7 2.6 reshape.99
  261.3 3.3 bitcast_convert_fusion
  264.6 4.1 copy.91
  268.7 3.2 multiply_reduce_fusion
  272.0 7.4 fusion.6
  279.3 3.6 copy.76
  283.0 6.8 fusion.1
  289.9 2.6 fusion.23
  300.2 3.9 fusion.24
  313.9 5.4 multiply_reduce_fusion.1
  319.3 302.8 %reduce-scatter.2.cloned.1.call-done = f32[32,1792]{1,0:T(8,128)} async-done(((f32[2048,1792]{1,0:T(8,128)}), f32[32,1792]{1,0:T(8,128)}) %reduce-scatter.2.cloned.1.call-update) | async-done | bytes 229392 | tf_op jit(solution)/shard_map/reduce_scatter | solution.py:127
  623.8 41.1 %all-to-all-start.1 = ((bf16[4,32,1792]{2,1,0:T(8,128)(2,1)}), bf16[4,32,1792]{2,1,0:T(8,128)(2,1)S(1)}, u32[]{:S(2)}, u32[]{:S(2)}) async-start(bf16[4,32,1792]{2,1,0:T(8,128)(2,1)} %broadcast_in_dim.47), calls=%async_computation.2 | async-start | bytes 917504 | tf_op jit(solution)/shard_map/all_to_all | solution.py:29
  668.3 2.1 multiply_reduce_fusion.2
  671.1 2.5 all-to-all-done.1
  674.9 6.5 all-reduce.1
  681.5 4.4 all-reduce.4
  685.9 13.9 %all-reduce = (f32[]{:T(128)}, f32[]{:T(128)}, f32[]{:T(128)}) all-reduce(f32[]{:T(128)} %get-tuple-element.32, f32[]{:T(128)} %get-tuple-element.33, f32[]{:T(128)} %get-tuple-element.34), channel_id=1, replica_groups=mesh['seq_0'=4,'seq_1'=2,'seq_2'=8,'dp_0'=2,'dp_1'=2] {'seq_2'}, use_global_device_ids=true, to_apply=%region_3.4 | all-reduce | flops 3 | bytes 24 | tf_op jit(solution)/shard_map/psum | solution.py:40
  699.8 5.9 all-reduce.3
  705.7 11.5 %all-reduce.2 = (f32[]{:T(128)}, f32[]{:T(128)}, f32[]{:T(128)}) all-reduce(f32[]{:T(128)} %get-tuple-element.29, f32[]{:T(128)} %get-tuple-element.30, f32[]{:T(128)} %get-tuple-element.31), channel_id=1, replica_groups=mesh['seq_0'=4,'seq_1'=2,'seq_2'=8,'dp_0'=2,'dp_1'=2] {'dp_1'}, use_global_device_ids=true, to_apply=%region_5.6 | all-reduce | flops 3 | bytes 24 | tf_op jit(solution)/shard_map/psum | solution.py:40
  723.8 2.2 fusion.11
  726.0 2.2 fusion.12
  (69 shorter events, 40.9 us)
Async XLA Ops:
  12.0 14.0 %copy-start.7 = (bf16[1,256,1024]{2,1,0:T(8,128)(2,1)S(1)}, bf16[1,256,1024]{2,1,0:T(8,128)(2,1)}, u32[]{:S(2)}) copy-start(bf16[1,256,1024]{2,1,0:T(8,128)(2,1)} %param.7) | copy-start | bytes 1572868
  12.0 21.9 %copy-start.8 = (bf16[1,256,1024]{2,1,0:T(8,128)(2,1)S(1)}, bf16[1,256,1024]{2,1,0:T(8,128)(2,1)}, u32[]{:S(2)}) copy-start(bf16[1,256,1024]{2,1,0:T(8,128)(2,1)} %param.8) | copy-start | bytes 1572868
  12.0 29.3 %copy-start.5 = (bf16[1,256,2048]{2,1,0:T(8,128)(2,1)S(1)}, bf16[1,256,2048]{2,1,0:T(8,128)(2,1)}, u32[]{:S(2)}) copy-start(bf16[1,256,2048]{2,1,0:T(8,128)(2,1)} %param.6) | copy-start | bytes 3145732
  12.0 240.2 %all-to-all-start = ((bf16[64,32,1792]{2,1,0:T(8,128)(2,1)}), bf16[64,32,1792]{2,1,0:T(8,128)(2,1)}, u32[]{:S(2)}, u32[]{:S(2)}) async-start(bf16[64,32,1792]{2,1,0:T(8,128)(2,1)} %stack.2), calls=%async_computation | async-start | bytes 14680064 | tf_op jit(solution)/shard_map/all_to_all | solution.py:93
  25.9 596.1 %reduce-scatter.2.cloned.1.call-start = ((), (), s32[]{:S(2)}) async-start(), calls=%async_computation.3 | async-start | bytes 14909440 | tf_op jit(solution)/shard_map/reduce_scatter | solution.py:127
  26.2 167.2 %collective-permute-start.1 = (bf16[256,1024]{0,1:T(8,128)(2,1)S(1)}, bf16[256,1024]{0,1:T(8,128)(2,1)}, u32[]{:S(2)}, u32[]{:S(2)}) collective-permute-start(bf16[256,1024]{0,1:T(8,128)(2,1)S(1)} %bitcast.113), channel_id=1, source_target_pairs={{0,4},{4,8},{8,12},{12,16},{16,20},{20,24},{24,28},{28,32},{32,36}... | collective-permute-start | bytes 1572872 | tf_op jit(solution)/shard_map/ppermute | solution.py:24
  29.9 180.1 %collective-permute-start = (bf16[256,1024]{0,1:T(8,128)(2,1)S(1)}, bf16[256,1024]{0,1:T(8,128)(2,1)}, u32[]{:S(2)}, u32[]{:S(2)}) collective-permute-start(bf16[256,1024]{0,1:T(8,128)(2,1)S(1)} %bitcast.114), channel_id=1, source_target_pairs={{0,8},{4,12},{8,16},{12,20},{16,24},{20,28},{24,32},{28,36},{32,40... | collective-permute-start | bytes 1572872 | tf_op jit(solution)/shard_map/ppermute | solution.py:24
  34.1 193.1 %collective-permute-start.3 = (bf16[256,1024]{0,1:T(8,128)(2,1)S(1)}, bf16[256,1024]{0,1:T(8,128)(2,1)}, u32[]{:S(2)}, u32[]{:S(2)}) collective-permute-start(bf16[256,1024]{0,1:T(8,128)(2,1)S(1)} %bitcast.110), channel_id=1, source_target_pairs={{0,4},{4,8},{8,12},{12,16},{16,20},{20,24},{24,28},{28,32},{32,36}... | collective-permute-start | bytes 1572872 | tf_op jit(solution)/shard_map/ppermute | solution.py:24
  39.2 204.6 %collective-permute-start.2 = (bf16[256,1024]{0,1:T(8,128)(2,1)S(1)}, bf16[256,1024]{0,1:T(8,128)(2,1)}, u32[]{:S(2)}, u32[]{:S(2)}) collective-permute-start(bf16[256,1024]{0,1:T(8,128)(2,1)S(1)} %bitcast.111), channel_id=1, source_target_pairs={{0,8},{4,12},{8,16},{12,20},{16,24},{20,28},{24,32},{28,36},{32,40... | collective-permute-start | bytes 1572872 | tf_op jit(solution)/shard_map/ppermute | solution.py:24
  41.8 204.0 %copy-start.1 = (bf16[1,256,2048]{1,2,0:T(8,128)(2,1)}, bf16[1,256,2048]{1,2,0:T(8,128)(2,1)S(1)}, u32[]{:S(2)}) copy-start(bf16[1,256,2048]{1,2,0:T(8,128)(2,1)S(1)} %copy.102) | copy-start | bytes 3145732
  42.0 205.8 %copy-start.9 = (bf16[256,4,256]{2,0,1:T(8,128)(2,1)}, bf16[256,4,256]{2,0,1:T(8,128)(2,1)S(1)}, u32[]{:S(2)}) copy-start(bf16[256,4,256]{2,0,1:T(8,128)(2,1)S(1)} %copy.59) | copy-start | bytes 1572868
  194.7 53.1 %copy-start.10 = (bf16[256,4,256]{2,0,1:T(8,128)(2,1)}, bf16[256,4,256]{2,0,1:T(8,128)(2,1)S(1)}, u32[]{:S(2)}) copy-start(bf16[256,4,256]{2,0,1:T(8,128)(2,1)S(1)} %copy.58) | copy-start | bytes 1572868
  211.2 36.6 %copy-start.11 = (bf16[256,4,256]{2,0,1:T(8,128)(2,1)}, bf16[256,4,256]{2,0,1:T(8,128)(2,1)S(1)}, u32[]{:S(2)}) copy-start(bf16[256,4,256]{2,0,1:T(8,128)(2,1)S(1)} %copy.57) | copy-start | bytes 1572868
  247.8 2.6 copy-start
  268.7 3.2 copy-start.6
  283.0 6.9 copy-start.2
  289.9 2.6 copy-start.3
  295.6 369.3 %collective-permute-start.5 = (bf16[256,1024]{1,0:T(8,128)(2,1)}, bf16[256,1024]{1,0:T(8,128)(2,1)}, u32[]{:S(2)}, u32[]{:S(2)}) collective-permute-start(bf16[256,1024]{1,0:T(8,128)(2,1)} %copy.75), channel_id=1, source_target_pairs={{8,0},{12,4},{16,8},{20,12},{24,16},{28,20},{32,24},{36,28},{40,32... | collective-permute-start | bytes 1572872 | tf_op jit(solution)/shard_map/ppermute | solution.py:24
  298.9 366.0 %collective-permute-start.4 = (bf16[256,1024]{1,0:T(8,128)(2,1)}, bf16[256,1024]{1,0:T(8,128)(2,1)}, u32[]{:S(2)}, u32[]{:S(2)}) collective-permute-start(bf16[256,1024]{1,0:T(8,128)(2,1)} %copy.73), channel_id=1, source_target_pairs={{4,0},{8,4},{12,8},{16,12},{20,16},{24,20},{28,24},{32,28},{36,32}... | collective-permute-start | bytes 1572872 | tf_op jit(solution)/shard_map/ppermute | solution.py:24
  307.6 360.7 %collective-permute-start.7 = (bf16[256,1024]{1,0:T(8,128)(2,1)}, bf16[256,1024]{1,0:T(8,128)(2,1)}, u32[]{:S(2)}, u32[]{:S(2)}) collective-permute-start(bf16[256,1024]{1,0:T(8,128)(2,1)} %copy.80), channel_id=1, source_target_pairs={{8,0},{12,4},{16,8},{20,12},{24,16},{28,20},{32,24},{36,28},{40,32... | collective-permute-start | bytes 1572872 | tf_op jit(solution)/shard_map/ppermute | solution.py:24
  312.6 355.7 %collective-permute-start.6 = (bf16[256,1024]{1,0:T(8,128)(2,1)}, bf16[256,1024]{1,0:T(8,128)(2,1)S(1)}, u32[]{:S(2)}, u32[]{:S(2)}) collective-permute-start(bf16[256,1024]{1,0:T(8,128)(2,1)} %copy.78), channel_id=1, source_target_pairs={{4,0},{8,4},{12,8},{16,12},{20,16},{24,20},{28,24},{32,28},{36,32}... | collective-permute-start | bytes 1572872 | tf_op jit(solution)/shard_map/ppermute | solution.py:24
  623.8 49.8 %all-to-all-start.1 = ((bf16[4,32,1792]{2,1,0:T(8,128)(2,1)}), bf16[4,32,1792]{2,1,0:T(8,128)(2,1)S(1)}, u32[]{:S(2)}, u32[]{:S(2)}) async-start(bf16[4,32,1792]{2,1,0:T(8,128)(2,1)} %broadcast_in_dim.47), calls=%async_computation.2 | async-start | bytes 917504 | tf_op jit(solution)/shard_map/all_to_all | solution.py:29
  668.3 50.9 %copy-start.4 = (bf16[256,1024]{1,0:T(8,128)(2,1)}, bf16[256,1024]{1,0:T(8,128)(2,1)S(1)}, u32[]{:S(2)}) copy-start(bf16[256,1024]{1,0:T(8,128)(2,1)S(1)} %collective-permute-done.6) | copy-start | bytes 1572868
Sparse Core Ops, SparseCore 0:
  279.5 342.5 reduce-scatter.1
